TPU v7x, 32 devices: a whole 2x2x4 slice. The times are simulated.
32 devices in a mesh: row: 8 (over z, core), col: 4 (over y, x).
Axes of the slice: x: 2, y: 2, z: 4, core: 2. Of those that a mesh axis runs over, the one named last changes fastest.
Arguments:
- x_fwd: bfloat16 [512, 6144], P('row', 'col'), may hold values from -6 to 6
- x_bwd: bfloat16 [512, 6144], P('row', 'col'), may hold values from -6 to 6
- grad_out: bfloat16 [512, 6144], P('row', 'col'), may hold values from -1.5 to 1.5
- gain: float32 [6144], P('col'), may hold values from 0.1 to 1.9
- w_up: bfloat16 [6144, 12288], P('col', 'row'), may hold values from -0.078125 to 0.078125
- w_down: bfloat16 [12288, 6144], P('row', 'col'), may hold values from -0.0546875 to 0.0546875
Outputs:
- y_fwd: bfloat16 [512, 6144], P('row', 'col')
- dx_bwd: bfloat16 [512, 6144], P('row', 'col')
- step_up: float32 [6144, 12288], P('col', 'row')
- step_down: float32 [12288, 6144], P('row', 'col')
- step_gain: float32 [6144], P('col')
- grad_rms: float32 [], replicated
All inputs are finite; a program needn't handle non-finite values.
Results may differ from a plain program's by a relative error of at most 0.0017.
The roundings to bfloat16 on the way count: a program that leaves them out, or rounds other values in their place, can miss the bound.
Values may be sent and summed in bfloat16 or wider, within the bound.
A program may use at most 128 MiB of HBM per device.

v0:
```python
import math
import jax
import jax.numpy as jnp
from jax import lax
from jax.sharding import PartitionSpec as P

D = 6144
FF = 12288
eps = 1e-06
clip_share = 0.25


def erf_gelu(value):
    return 0.5 * value * (1.0 + lax.erf(value * 0.7071067811865476))


def gelu_slope(value):
    return (
        0.5 * (1.0 + lax.erf(value * 0.7071067811865476))
        + value * jnp.exp(-0.5 * value * value) * 0.3989422804014327
    )


def contract(left, right, left_dim, right_dim):
    return lax.dot_general(
        left, right, (((left_dim,), (right_dim,)), ((), ())), preferred_element_type=jnp.float32
    )


def row_sums(tokens):
    values = tokens.astype(jnp.float32)
    return (jnp.sum(values, -1), jnp.sum(values * values, -1))


def normalize(tokens, first, second):
    values = tokens.astype(jnp.float32)
    centre = first / D
    spread = second / D - centre * centre
    inv_scale = lax.rsqrt(spread + eps)
    return ((values - centre[:, None]) * inv_scale[:, None], inv_scale)


def up_both(normed_a, normed_b, w_up):
    full_a, full_b = (
        lax.all_gather(normed_a, "row", axis=0, tiled=True),
        lax.all_gather(normed_b, "row", axis=0, tiled=True),
    )
    width = w_up.shape[1]
    summed = lax.psum_scatter(
        jnp.concatenate(
            [
                jnp.dot(full_a, w_up, preferred_element_type=jnp.float32),
                jnp.dot(full_b, w_up, preferred_element_type=jnp.float32),
            ],
            1,
        ),
        "col",
        scatter_dimension=0,
        tiled=True,
    )
    return (summed[:, :width], summed[:, width:], full_b)


def on_device(x_fwd, x_bwd, grad_out, gain, w_up, w_down):
    first_a, second_a = row_sums(x_fwd)
    first_b, second_b = row_sums(x_bwd)
    first_a, second_a, first_b, second_b = lax.psum((first_a, second_a, first_b, second_b), "col")
    centred_a, _ = normalize(x_fwd, first_a, second_a)
    centred_b, inv_scale = normalize(x_bwd, first_b, second_b)
    normed_a = (centred_a * gain).astype(jnp.bfloat16)
    normed_b = (centred_b * gain).astype(jnp.bfloat16)
    pre_a, pre_b, normed_full = up_both(normed_a, normed_b, w_up)
    hidden_a = erf_gelu(pre_a).astype(jnp.bfloat16)
    output_part = jnp.dot(
        lax.all_gather(hidden_a, "col", axis=0, tiled=True),
        w_down,
        preferred_element_type=jnp.float32,
    )
    output_sum = lax.psum_scatter(output_part, "row", scatter_dimension=0, tiled=True)
    y_fwd = (x_fwd.astype(jnp.float32) + output_sum).astype(jnp.bfloat16)
    hidden_b = erf_gelu(pre_b).astype(jnp.bfloat16)
    grad_full = lax.all_gather(grad_out, "row", axis=0, tiled=True)
    grad_hidden = lax.psum_scatter(
        contract(grad_full, w_down, 1, 1), "col", scatter_dimension=0, tiled=True
    )
    grad_pre = (grad_hidden * gelu_slope(pre_b)).astype(jnp.bfloat16)
    hidden_piece = lax.all_gather(hidden_b, "col", axis=0, tiled=True)
    pre_piece = lax.all_gather(grad_pre, "col", axis=0, tiled=True)
    down_total = contract(hidden_piece, grad_full, 0, 0)
    up_total = contract(normed_full, pre_piece, 0, 0)
    input_total = contract(pre_piece, w_up, 1, 1)
    grad_normed = lax.psum_scatter(input_total, "row", scatter_dimension=0, tiled=True)
    scaled = grad_normed * gain
    first_back = jnp.sum(scaled, -1)
    second_back = jnp.sum(scaled * centred_b, -1)
    first_back, second_back = lax.psum((first_back, second_back), "col")
    dx_bwd = (
        grad_out.astype(jnp.float32)
        + inv_scale[:, None]
        * (scaled - first_back[:, None] / D - centred_b * (second_back[:, None] / D))
    ).astype(jnp.bfloat16)
    gain_part = jnp.sum(grad_normed * centred_b, 0)
    weight_squares = jnp.sum(up_total * up_total) + jnp.sum(down_total * down_total)
    g_gain = lax.psum(gain_part, "row")
    first_row = (lax.axis_index("row") == 0).astype(jnp.float32)
    total = lax.psum(weight_squares + first_row * jnp.sum(g_gain * g_gain), ("row", "col"))
    param_count = 2 * D * FF + D
    norm_value = jnp.sqrt(total)
    grad_rms = norm_value / math.sqrt(param_count)
    factor = jnp.minimum(1.0, clip_share * math.sqrt(param_count) / norm_value)
    return (y_fwd, dx_bwd, up_total * factor, down_total * factor, g_gain * factor, grad_rms)


def solution(mesh):
    placed = (
        P("row", "col"),
        P("row", "col"),
        P("row", "col"),
        P("col"),
        P("col", "row"),
        P("row", "col"),
    )
    return jax.shard_map(
        on_device,
        mesh=mesh,
        in_specs=placed,
        out_specs=(
            P("row", "col"),
            P("row", "col"),
            P("col", "row"),
            P("row", "col"),
            P("col"),
            P(),
        ),
        check_vma=False,
    )
```

profile of v0, /device:TPU:0, one launch (start us, length us, event | category | flops | bytes accessed | tf_op | source)
XLA Modules:
  0.0 446.6 jit_solution(12459251885347289089)
XLA Ops:
  7.2 0.0 all-gather.13.cloned.1.call-start
  7.2 0.7 all-gather.13.cloned.1.call-update
  7.9 0.0 all-gather.7.cloned.1.call-start
  7.9 1.1 convert_reduce_fusion
  9.0 1.1 convert_reduce_fusion.1
  10.1 11.4 %all-reduce.1 = (f32[64]{0:T(128)S(1)}, f32[64]{0:T(128)S(1)}, f32[64]{0:T(128)S(1)}, f32[64]{0:T(128)S(1)}) all-reduce(f32[64]{0:T(128)S(1)} %get-tuple-element.12, f32[64]{0:T(128)S(1)} %get-tuple-element.11, f32[64]{0:T(128)S(1)} %get-tuple-element.10, f32[64]{0:T(128)S(1)} %get-tuple-element.9), channel_id=1, replica_groups=mesh['row'=8,'col'=4] {'col'}, use_global_device_ids=true, to_apply=%region_7.0 | all-reduce | flops 256 | bytes 2048 | tf_op jit(solution)/shard_map/psum | solution.py:67
  21.5 2.0 fusion.21
  23.6 0.0 all-gather.9.cloned.1.call-start
  23.6 0.7 all-gather.9.cloned.1.call-update
  24.3 0.0 reduce-scatter.9.cloned.1.call-start
  24.4 13.3 %all-gather.13.cloned.1.call-done = bf16[512,1536]{1,0:T(8,128)(2,1)} async-done(((bf16[64,1536]{1,0:T(8,128)(2,1)}), bf16[512,1536]{1,0:T(8,128)(2,1)}) %all-gather.13.cloned.1.call-update) | async-done | bytes 1572880 | tf_op jit(solution)/shard_map/all_gather | solution.py:82
  37.6 7.1 %fusion.27 = f32[512,1536]{1,0:T(8,128)} fusion(bf16[512,1536]{1,0:T(8,128)(2,1)} %all-gather.13.cloned.1.call-done, bf16[1536,1536]{1,0:T(8,128)(2,1)} %param.11), kind=kOutput, calls=%fused_computation.52 | convolution fusion | flops 2415919104 | bytes 9437184 | tf_op jit(solution)/shard_map/dot_general | solution.py:25
  44.8 0.0 reduce-scatter.5.cloned.1.call-start
  44.8 19.4 %all-gather.7.cloned.1.call-done = bf16[512,1536]{1,0:T(8,128)(2,1)} async-done(((bf16[64,1536]{1,0:T(8,128)(2,1)}), bf16[512,1536]{1,0:T(8,128)(2,1)}) %all-gather.7.cloned.1.call-update) | async-done | bytes 1572880 | tf_op jit(solution)/shard_map/all_gather | solution.py:45
  64.3 4.9 %fusion.24 = f32[512,1536]{1,0:T(8,128)S(1)} fusion(bf16[512,1536]{1,0:T(8,128)(2,1)} %all-gather.7.cloned.1.call-done, bf16[1536,1536]{1,0:T(8,128)(2,1)} %param.10), kind=kOutput, calls=%fused_computation.49 | convolution fusion | flops 2415919104 | bytes 9437184 | tf_op jit(solution)/shard_map/dot_general | solution.py:52
  69.2 21.7 %all-gather.9.cloned.1.call-done = bf16[512,1536]{1,0:T(8,128)(2,1)} async-done(((bf16[64,1536]{1,0:T(8,128)(2,1)}), bf16[512,1536]{1,0:T(8,128)(2,1)}) %all-gather.9.cloned.1.call-update) | async-done | bytes 1572880 | tf_op jit(solution)/shard_map/all_gather | solution.py:46
  90.9 4.9 %fusion.25 = f32[512,1536]{1,0:T(8,128)S(1)} fusion(bf16[512,1536]{1,0:T(8,128)(2,1)} %all-gather.9.cloned.1.call-done, bf16[1536,1536]{1,0:T(8,128)(2,1)} %param.10), kind=kOutput, calls=%fused_computation.50 | convolution fusion | flops 2415919104 | bytes 9437184 | tf_op jit(solution)/shard_map/dot_general | solution.py:53
  95.9 3.3 pad_maximum_fusion
  99.1 0.0 all-gather.15.cloned.1.call-start
  99.2 38.2 %reduce-scatter.9.cloned.1.call-done = f32[128,1536]{1,0:T(8,128)} async-done(((f32[512,1536]{1,0:T(8,128)}), f32[128,1536]{1,0:T(8,128)}) %reduce-scatter.9.cloned.1.call-update) | async-done | bytes 786448 | tf_op jit(solution)/shard_map/reduce_scatter | solution.py:83
  137.4 73.5 %reduce-scatter.5.cloned.1.call-done = f32[128,3072]{1,0:T(8,128)} async-done(((f32[512,3072]{1,0:T(8,128)}), f32[128,3072]{1,0:T(8,128)}) %reduce-scatter.5.cloned.1.call-update) | async-done | bytes 1572880 | tf_op jit(solution)/shard_map/reduce_scatter | solution.py:49
  210.9 3.0 multiply_convert_fusion
  213.9 0.0 all-gather.11.cloned.1.call-start
  214.0 0.7 all-gather.11.cloned.1.call-update
  214.7 0.0 all-gather.17.cloned.1.call-start
  214.7 0.7 all-gather.17.cloned.1.call-update
  215.4 0.0 reduce-scatter.11.cloned.1.call-start
  215.5 29.5 %all-gather.15.cloned.1.call-done = bf16[512,1536]{1,0:T(8,128)(2,1)} async-done(((bf16[128,1536]{1,0:T(8,128)(2,1)}), bf16[512,1536]{1,0:T(8,128)(2,1)}) %all-gather.15.cloned.1.call-update) | async-done | bytes 1572880 | tf_op jit(solution)/shard_map/all_gather | solution.py:88
  244.9 7.1 %fusion.28 = f32[512,1536]{1,0:T(8,128)} fusion(bf16[512,1536]{1,0:T(8,128)(2,1)} %all-gather.15.cloned.1.call-done, bf16[1536,1536]{1,0:T(8,128)(2,1)} %param.10), kind=kOutput, calls=%fused_computation.53 | convolution fusion | flops 2415919104 | bytes 9437184 | tf_op jit(solution)/shard_map/dot_general | solution.py:25
  252.1 0.2 reduce-scatter.7.cloned.1.call-start
  252.3 25.3 %all-gather.11.cloned.1.call-done = bf16[512,1536]{1,0:T(8,128)(2,1)} async-done(((bf16[128,1536]{1,0:T(8,128)(2,1)}), bf16[512,1536]{1,0:T(8,128)(2,1)}) %all-gather.11.cloned.1.call-update) | async-done | bytes 1572880 | tf_op jit(solution)/shard_map/all_gather | solution.py:75
  277.6 7.1 %fusion.26 = f32[512,1536]{1,0:T(8,128)} fusion(bf16[512,1536]{1,0:T(8,128)(2,1)} %all-gather.11.cloned.1.call-done, bf16[1536,1536]{1,0:T(8,128)(2,1)} %param.11), kind=kOutput, calls=%fused_computation.51 | convolution fusion | flops 2415919104 | bytes 9437184 | tf_op jit(solution)/shard_map/dot_general | solution.py:74
  284.8 1.4 copy-done.5
  286.2 0.5 copy-done.6
  286.7 6.0 %multiply_reduce_fusion.1 = (f32[]{:T(128)}, f32[1536,1536]{1,0:T(8,128)}) fusion(bf16[512,1536]{1,0:T(8,128)(2,1)S(1)} %copy-done.5, bf16[512,1536]{1,0:T(8,128)(2,1)S(1)} %copy-done.6), kind=kOutput, calls=%fused_computation.1 | convolution fusion | flops 2420637696 | bytes 12582916 | tf_op jit(solution)/shard_map/dot_general | solution.py:25
  292.7 18.2 %all-gather.17.cloned.1.call-done = bf16[512,1536]{1,0:T(8,128)(2,1)} async-done(((bf16[128,1536]{1,0:T(8,128)(2,1)}), bf16[512,1536]{1,0:T(8,128)(2,1)}) %all-gather.17.cloned.1.call-update) | async-done | bytes 1572880 | tf_op jit(solution)/shard_map/all_gather | solution.py:87
  310.9 8.9 %multiply_reduce_fusion = (f32[]{:T(128)}, f32[1536,1536]{1,0:T(8,128)}) fusion(bf16[512,1536]{1,0:T(8,128)(2,1)} %all-gather.17.cloned.1.call-done, bf16[512,1536]{1,0:T(8,128)(2,1)} %all-gather.13.cloned.1.call-done), kind=kOutput, calls=%fused_computation | convolution fusion | flops 2420637696 | bytes 12582916 | tf_op jit(solution)/shard_map/dot_general | solution.py:25
  321.1 32.5 %reduce-scatter.11.cloned.1.call-done = f32[64,1536]{1,0:T(8,128)} async-done(((f32[512,1536]{1,0:T(8,128)}), f32[64,1536]{1,0:T(8,128)}) %reduce-scatter.11.cloned.1.call-update) | async-done | bytes 393232 | tf_op jit(solution)/shard_map/reduce_scatter | solution.py:92
  353.6 1.4 fusion.17
  355.0 16.1 %psum.62 = f32[1536]{0:T(1024)S(1)} all-reduce(f32[1536]{0:T(1024)S(1)} %get-tuple-element.6), channel_id=1, replica_groups=mesh['row'=8,'col'=4] {'row'}, use_global_device_ids=true, to_apply=%region_19.0 | all-reduce | flops 1536 | bytes 12288 | tf_op jit(solution)/shard_map/psum | solution.py:104
  371.1 0.6 multiply_reduce_fusion.3
  372.3 38.8 %psum.63 = f32[]{:T(128)} all-reduce(f32[]{:T(128)S(6)} %add.60), channel_id=1, replica_groups=mesh['row'=8,'col'=4] {'row','col'}, use_global_device_ids=true, to_apply=%region_21.0 | all-reduce | flops 1 | bytes 8 | tf_op jit(solution)/shard_map/psum | solution.py:106
  411.9 9.9 %all-reduce = (f32[64]{0:T(128)S(1)}, f32[64]{0:T(128)S(1)}) all-reduce(f32[64]{0:T(128)S(1)} %get-tuple-element.7, f32[64]{0:T(128)S(1)} %get-tuple-element.8), channel_id=1, replica_groups=mesh['row'=8,'col'=4] {'col'}, use_global_device_ids=true, to_apply=%region_15.0 | all-reduce | flops 128 | bytes 1024 | tf_op jit(solution)/shard_map/psum | solution.py:96
  421.8 0.6 broadcast_multiply_fusion.2
  422.5 8.7 %broadcast_multiply_fusion = f32[1536,1536]{1,0:T(8,128)} fusion(f32[1536,1536]{1,0:T(8,128)} %get-tuple-element.31, f32[]{:T(128)S(6)} %min.3), kind=kLoop, calls=%fused_computation.3 | loop fusion | flops 2359296 | bytes 18874372 | tf_op jit(solution)/shard_map/mul | solution.py:111
  431.2 4.8 %broadcast_multiply_fusion.1 = f32[1536,1536]{1,0:T(8,128)} fusion(f32[1536,1536]{1,0:T(8,128)S(1)} %bitcast.15, f32[]{:T(128)S(6)} %min.3), kind=kLoop, calls=%fused_computation.4 | loop fusion | flops 2359296 | bytes 18874372 | tf_op jit(solution)/shard_map/mul | solution.py:111
  436.0 1.7 fusion.23
  437.7 0.9 fusion.16
  (29 shorter events, 0.2 us)
Async XLA Ops:
  7.2 30.5 %all-gather.13.cloned.1.call-start = ((), (), s32[]{:S(2)}) async-start(), calls=%async_computation.9 | async-start | bytes 1769472 | tf_op jit(solution)/shard_map/all_gather | solution.py:82
  7.9 56.4 %all-gather.7.cloned.1.call-start = ((), (), s32[]{:S(2)}) async-start(), calls=%async_computation.4 | async-start | bytes 1769472 | tf_op jit(solution)/shard_map/all_gather | solution.py:45
  23.6 67.3 %all-gather.9.cloned.1.call-start = ((), (), s32[]{:S(2)}) async-start(), calls=%async_computation.5 | async-start | bytes 1769472 | tf_op jit(solution)/shard_map/all_gather | solution.py:46
  24.3 113.1 %reduce-scatter.9.cloned.1.call-start = ((), (), s32[]{:S(2)}) async-start(), calls=%async_computation.10 | async-start | bytes 3932160 | tf_op jit(solution)/shard_map/reduce_scatter | solution.py:83
  44.8 166.1 %reduce-scatter.5.cloned.1.call-start = ((), (), s32[]{:S(2)}) async-start(), calls=%async_computation.6 | async-start | bytes 7864320 | tf_op jit(solution)/shard_map/reduce_scatter | solution.py:49
  99.1 145.8 %all-gather.15.cloned.1.call-start = ((), (), s32[]{:S(2)}) async-start(), calls=%async_computation.11 | async-start | bytes 1966080 | tf_op jit(solution)/shard_map/all_gather | solution.py:88
  213.9 63.7 %all-gather.11.cloned.1.call-start = ((), (), s32[]{:S(2)}) async-start(), calls=%async_computation.7 | async-start | bytes 1966080 | tf_op jit(solution)/shard_map/all_gather | solution.py:75
  214.7 96.2 %all-gather.17.cloned.1.call-start = ((), (), s32[]{:S(2)}) async-start(), calls=%async_computation.13 | async-start | bytes 1966080 | tf_op jit(solution)/shard_map/all_gather | solution.py:87
  215.4 138.2 %reduce-scatter.11.cloned.1.call-start = ((), (), s32[]{:S(2)}) async-start(), calls=%async_computation.12 | async-start | bytes 3538944 | tf_op jit(solution)/shard_map/reduce_scatter | solution.py:92
  252.1 183.9 %reduce-scatter.7.cloned.1.call-start = ((), (), s32[]{:S(2)}) async-start(), calls=%async_computation.8 | async-start | bytes 3538944 | tf_op jit(solution)/shard_map/reduce_scatter | solution.py:79
  284.8 1.4 copy-start.5
  284.8 1.9 copy-start.6
  292.7 60.9 %copy-start = (bf16[64,1536]{1,0:T(8,128)(2,1)S(1)}, bf16[64,1536]{1,0:T(8,128)(2,1)}, u32[]{:S(2)}) copy-start(bf16[64,1536]{1,0:T(8,128)(2,1)} %param.7) | copy-start | bytes 589828
  292.7 60.9 %copy-start.4 = (f32[1536]{0:T(1024)S(1)}, f32[1536]{0:T(1024)}, u32[]{:S(2)}) copy-start(f32[1536]{0:T(1024)} %param.9) | copy-start | bytes 18436
  353.6 77.5 %slice-start = ((s8[9437184]{0:T(1024)(128)(4,1)}), s8[1048576]{0:T(1024)(128)(4,1)S(1)}, s32[]{:S(2)}) async-start(s8[9437184]{0:T(1024)(128)(4,1)} %bitcast.14), calls=%async_computation.14 | async-start | bytes 2097152
  422.4 8.7 %slice-start.1 = ((s8[9437184]{0:T(1024)(128)(4,1)}), s8[4194304]{0:T(1024)(128)(4,1)S(1)}, s32[]{:S(2)}) async-start(s8[9437184]{0:T(1024)(128)(4,1)} %bitcast.14), calls=%async_computation.15 | async-start | bytes 8388608
  422.4 8.7 %slice-start.2 = ((s8[9437184]{0:T(1024)(128)(4,1)}), s8[4194304]{0:T(1024)(128)(4,1)S(1)}, s32[]{:S(2)}) async-start(s8[9437184]{0:T(1024)(128)(4,1)} %bitcast.14), calls=%async_computation.16 | async-start | bytes 8388608
  431.1 4.8 %copy-start.1 = (bf16[64,1536]{1,0:T(8,128)(2,1)S(1)}, bf16[64,1536]{1,0:T(8,128)(2,1)}, u32[]{:S(2)}) copy-start(bf16[64,1536]{1,0:T(8,128)(2,1)} %param.6) | copy-start | bytes 589828
  431.2 6.5 %copy-start.2 = (f32[64,1536]{1,0:T(8,128)S(1)}, f32[64,1536]{1,0:T(8,128)}, u32[]{:S(2)}) copy-start(f32[64,1536]{1,0:T(8,128)} %reduce-scatter.11.cloned.1.call-done) | copy-start | bytes 1179652
  431.2 6.5 %copy-start.3 = (bf16[64,1536]{1,0:T(8,128)(2,1)S(1)}, bf16[64,1536]{1,0:T(8,128)(2,1)}, u32[]{:S(2)}) copy-start(bf16[64,1536]{1,0:T(8,128)(2,1)} %param.8) | copy-start | bytes 589828
Sparse Core Ops, SparseCore 0:
  9.6 27.9 all-gather.12
  39.8 24.3 all-gather.6
  66.5 24.3 all-gather.8
  94.3 43.0 reduce-scatter.8
  140.8 70.0 reduce-scatter.4
  214.0 30.8 all-gather.14
  246.8 30.8 all-gather.10
  280.0 30.8 all-gather.16
  313.2 40.3 reduce-scatter.10
  355.8 40.2 reduce-scatter.6
where the time goes:
time: 447 us
  waiting for transfers between devices  274 us (61%)
  blocking collectives  76.2 us (17%)
  matrix products  46.1 us (10%)
  other arithmetic  29.2 us (7%)
  between operations  18.1 us (4%)
    reduce_scatter x1, waiting for transfers between devices, up_both(): lax.psum_scatter(jnp.concatenate([jnp.dot(full_a, w_up, preferred_element...  73.5 us
    psum x1, blocking collectives, on_device(): lax.psum(weight_squares + first_row * jnp.sum(g_gain * g_gain), ('row', '...  38.8 us
    reduce_scatter x1, waiting for transfers between devices, on_device(): lax.psum_scatter(contract(grad_full, w_down, 1, 1), 'col', scatter_dimens...  38.2 us
    reduce_scatter x1, waiting for transfers between devices, on_device(): lax.psum_scatter(input_total, 'row', scatter_dimension=0, tiled=True)  32.5 us
    all_gather x1, waiting for transfers between devices, on_device(): pre_piece = lax.all_gather(grad_pre, 'col', axis=0, tiled=True)  29.5 us
    dot_general x4, matrix products, contract(): lax.dot_general(left, right, (((left_dim,), (right_dim,)), ((), ())), pre...  29.2 us
    all_gather x1, waiting for transfers between devices, on_device(): lax.all_gather(hidden_a, 'col', axis=0, tiled=True)  25.3 us
    all_gather x1, waiting for transfers between devices, up_both(): lax.all_gather(normed_b, 'row', axis=0, tiled=True)  21.7 us
  transfers between devices with their start and end apart: 10, of which 9 were waited for; matrix products, arithmetic and copies ran while one was open for 16% of the time, Pallas kernels for 0%

commit v1 on v0

--- a/solution.py
+++ b/solution.py
@@ -84,8 +84,13 @@
         contract(grad_full, w_down, 1, 1), "col", scatter_dimension=0, tiled=True
     )
     grad_pre = (grad_hidden * gelu_slope(pre_b)).astype(jnp.bfloat16)
-    hidden_piece = lax.all_gather(hidden_b, "col", axis=0, tiled=True)
-    pre_piece = lax.all_gather(grad_pre, "col", axis=0, tiled=True)
+    hidden_piece, pre_piece = jnp.split(
+        lax.all_gather(
+            jnp.concatenate([hidden_b, grad_pre], axis=1), axis_name="col", axis=0, tiled=True
+        ),
+        [hidden_b.shape[1]],
+        axis=1,
+    )
     down_total = contract(hidden_piece, grad_full, 0, 0)
     up_total = contract(normed_full, pre_piece, 0, 0)
     input_total = contract(pre_piece, w_up, 1, 1)

time: 447 us -> 465 us (1.040)
  waiting for transfers between devices: 274 us -> 295 us
    reduce_scatter x1, waiting for transfers between devices: 0.01 us -> 18.1 us  [on_device(): lax.psum_scatter(output_part, 'row', scatter_dimension=0, tiled=True)]
    all_gather x2 -> x1, waiting for transfers between devices: 47.6 us -> 38.9 us  [on_device(): lax.all_gather(jnp.concatenate([hidden_b, grad_pre], axis=1), axis_name='...]
    reduce_scatter x1, waiting for transfers between devices: 32.5 us -> 40.3 us  [on_device(): lax.psum_scatter(input_total, 'row', scatter_dimension=0, tiled=True)]
  transfers between devices with their start and end apart: 10 -> 9, of which waited for: 9 -> 9; matrix products, arithmetic and copies ran while one was open for 16% -> 12% of each run, Pallas kernels for 0% -> 0%
where the time goes in v1:
time: 465 us; the launch traced here: 464 us
  waiting for transfers between devices  295 us (63%)
  blocking collectives  73.5 us (16%)
  matrix products  45.1 us (10%)
  other arithmetic  30 us (6%)
  between operations  17.8 us (4%)
    reduce_scatter x1, waiting for transfers between devices, up_both(): lax.psum_scatter(jnp.concatenate([jnp.dot(full_a, w_up, preferred_element...  73.5 us
    reduce_scatter x1, waiting for transfers between devices, on_device(): lax.psum_scatter(input_total, 'row', scatter_dimension=0, tiled=True)  40.3 us
    all_gather x1, waiting for transfers between devices, on_device(): lax.all_gather(jnp.concatenate([hidden_b, grad_pre], axis=1), axis_name='...  38.9 us
    reduce_scatter x1, waiting for transfers between devices, on_device(): lax.psum_scatter(contract(grad_full, w_down, 1, 1), 'col', scatter_dimens...  38.2 us
    psum x1, blocking collectives, on_device(): lax.psum(weight_squares + first_row * jnp.sum(g_gain * g_gain), ('row', '...  36.9 us
    all_gather x1, waiting for transfers between devices, on_device(): lax.all_gather(hidden_a, 'col', axis=0, tiled=True)  29.9 us
    dot_general x4, matrix products, contract(): lax.dot_general(left, right, (((left_dim,), (right_dim,)), ((), ())), pre...  28.2 us
    all_gather x1, waiting for transfers between devices, up_both(): lax.all_gather(normed_b, 'row', axis=0, tiled=True)  21.7 us
  transfers between devices with their start and end apart: 9, of which 9 were waited for; matrix products, arithmetic and copies ran while one was open for 12% of the time, Pallas kernels for 0%

profile of v1, /device:TPU:0, one launch (start us, length us, event | category | flops | bytes accessed | tf_op | source)
XLA Modules:
  0.0 464.0 jit_solution(17538693833433128261)
XLA Ops:
  7.2 0.0 all-gather.12.cloned.1.call-start
  7.2 0.7 all-gather.12.cloned.1.call-update
  7.9 0.0 all-gather.6.cloned.1.call-start
  7.9 1.1 convert_reduce_fusion
  9.0 1.1 convert_reduce_fusion.1
  10.1 11.4 %all-reduce.1 = (f32[64]{0:T(128)S(1)}, f32[64]{0:T(128)S(1)}, f32[64]{0:T(128)S(1)}, f32[64]{0:T(128)S(1)}) all-reduce(f32[64]{0:T(128)S(1)} %get-tuple-element.12, f32[64]{0:T(128)S(1)} %get-tuple-element.11, f32[64]{0:T(128)S(1)} %get-tuple-element.10, f32[64]{0:T(128)S(1)} %get-tuple-element.9), channel_id=1, replica_groups=mesh['row'=8,'col'=4] {'col'}, use_global_device_ids=true, to_apply=%region_7.0 | all-reduce | flops 256 | bytes 2048 | tf_op jit(solution)/shard_map/psum | solution.py:67
  21.5 2.0 fusion.27
  23.6 0.0 all-gather.6.cloned.1.call-update
  23.6 0.0 all-gather.8.cloned.1.call-start
  23.6 0.7 all-gather.8.cloned.1.call-update
  24.3 0.0 reduce-scatter.9.cloned.1.call-start
  24.4 13.3 %all-gather.12.cloned.1.call-done = bf16[512,1536]{1,0:T(8,128)(2,1)} async-done(((bf16[64,1536]{1,0:T(8,128)(2,1)}), bf16[512,1536]{1,0:T(8,128)(2,1)}) %all-gather.12.cloned.1.call-update) | async-done | bytes 1572880 | tf_op jit(solution)/shard_map/all_gather | solution.py:82
  37.6 7.1 %fusion.33 = f32[512,1536]{1,0:T(8,128)} fusion(bf16[512,1536]{1,0:T(8,128)(2,1)} %all-gather.12.cloned.1.call-done, bf16[1536,1536]{1,0:T(8,128)(2,1)} %param.11), kind=kOutput, calls=%fused_computation.59 | convolution fusion | flops 2415919104 | bytes 9437184 | tf_op jit(solution)/shard_map/dot_general | solution.py:25
  44.8 0.0 reduce-scatter.9.cloned.1.call-update
  44.8 0.0 reduce-scatter.5.cloned.1.call-start
  44.8 19.4 %all-gather.6.cloned.1.call-done = bf16[512,1536]{1,0:T(8,128)(2,1)} async-done(((bf16[64,1536]{1,0:T(8,128)(2,1)}), bf16[512,1536]{1,0:T(8,128)(2,1)}) %all-gather.6.cloned.1.call-update) | async-done | bytes 1572880 | tf_op jit(solution)/shard_map/all_gather | solution.py:45
  64.3 4.9 %fusion.30 = f32[512,1536]{1,0:T(8,128)S(1)} fusion(bf16[512,1536]{1,0:T(8,128)(2,1)} %all-gather.6.cloned.1.call-done, bf16[1536,1536]{1,0:T(8,128)(2,1)} %param.10), kind=kOutput, calls=%fused_computation.56 | convolution fusion | flops 2415919104 | bytes 9437184 | tf_op jit(solution)/shard_map/dot_general | solution.py:52
  69.2 21.7 %all-gather.8.cloned.1.call-done = bf16[512,1536]{1,0:T(8,128)(2,1)} async-done(((bf16[64,1536]{1,0:T(8,128)(2,1)}), bf16[512,1536]{1,0:T(8,128)(2,1)}) %all-gather.8.cloned.1.call-update) | async-done | bytes 1572880 | tf_op jit(solution)/shard_map/all_gather | solution.py:46
  90.9 4.9 %fusion.31 = f32[512,1536]{1,0:T(8,128)S(1)} fusion(bf16[512,1536]{1,0:T(8,128)(2,1)} %all-gather.8.cloned.1.call-done, bf16[1536,1536]{1,0:T(8,128)(2,1)} %param.10), kind=kOutput, calls=%fused_computation.57 | convolution fusion | flops 2415919104 | bytes 9437184 | tf_op jit(solution)/shard_map/dot_general | solution.py:53
  95.9 3.3 pad_maximum_fusion
  99.1 0.0 reduce-scatter.5.cloned.1.call-update
  99.1 0.0 all-gather.10.cloned.1.call-start
  99.2 38.2 %reduce-scatter.9.cloned.1.call-done = f32[128,1536]{1,0:T(8,128)} async-done(((f32[512,1536]{1,0:T(8,128)}), f32[128,1536]{1,0:T(8,128)}) %reduce-scatter.9.cloned.1.call-update) | async-done | bytes 786448 | tf_op jit(solution)/shard_map/reduce_scatter | solution.py:83
  137.4 73.5 %reduce-scatter.5.cloned.1.call-done = f32[128,3072]{1,0:T(8,128)} async-done(((f32[512,3072]{1,0:T(8,128)}), f32[128,3072]{1,0:T(8,128)}) %reduce-scatter.5.cloned.1.call-update) | async-done | bytes 1572880 | tf_op jit(solution)/shard_map/reduce_scatter | solution.py:49
  210.9 2.9 multiply_convert_fusion
  213.8 0.0 all-gather.14.cloned.1.call-start
  213.8 1.0 pad_maximum_fusion.1
  214.8 0.0 reduce-scatter.7.cloned.1.call-start
  214.9 29.9 %all-gather.10.cloned.1.call-done = bf16[512,1536]{1,0:T(8,128)(2,1)} async-done(((bf16[128,1536]{1,0:T(8,128)(2,1)}), bf16[512,1536]{1,0:T(8,128)(2,1)}) %all-gather.10.cloned.1.call-update) | async-done | bytes 1572880 | tf_op jit(solution)/shard_map/all_gather | solution.py:75
  244.8 7.1 %fusion.32 = f32[512,1536]{1,0:T(8,128)} fusion(bf16[512,1536]{1,0:T(8,128)(2,1)} %all-gather.10.cloned.1.call-done, bf16[1536,1536]{1,0:T(8,128)(2,1)} %param.11), kind=kOutput, calls=%fused_computation.58 | convolution fusion | flops 2415919104 | bytes 9437184 | tf_op jit(solution)/shard_map/dot_general | solution.py:74
  251.9 0.2 reduce-scatter.11.cloned.1.call-start
  252.1 38.9 %all-gather.14.cloned.1.call-done = bf16[512,3072]{1,0:T(8,128)(2,1)} async-done(((bf16[128,3072]{1,0:T(8,128)(2,1)}), bf16[512,3072]{1,0:T(8,128)(2,1)}) %all-gather.14.cloned.1.call-update) | async-done | bytes 3145744 | tf_op jit(solution)/shard_map/all_gather | solution.py:88
  291.1 7.2 %fusion.4 = f32[512,1536]{1,0:T(8,128)} fusion(bf16[1536,1536]{1,0:T(8,128)(2,1)} %param.10, bf16[512,3072]{1,0:T(8,128)(2,1)} %all-gather.14.cloned.1.call-done), kind=kOutput, calls=%fused_computation.9 | convolution fusion | flops 2415919104 | bytes 9437184 | tf_op jit(solution)/shard_map/dot_general | solution.py:25
  298.2 2.1 copy-done.5
  300.4 7.6 %multiply_reduce_fusion.1 = (f32[]{:T(128)}, f32[1536,1536]{1,0:T(8,128)}) fusion(bf16[512,1536]{1,0:T(8,128)(2,1)} %all-gather.8.cloned.1.call-done, bf16[512,3072]{1,0:T(8,128)(2,1)S(1)} %copy-done.5), kind=kOutput, calls=%fused_computation.1 | convolution fusion | flops 2420637696 | bytes 12582916 | tf_op jit(solution)/shard_map/dot_general | solution.py:25
  308.0 6.3 %multiply_reduce_fusion = (f32[]{:T(128)}, f32[1536,1536]{1,0:T(8,128)}) fusion(bf16[512,1536]{1,0:T(8,128)(2,1)S(1)} %copy-done.7, bf16[512,3072]{1,0:T(8,128)(2,1)S(1)} %copy-done.6), kind=kOutput, calls=%fused_computation | convolution fusion | flops 2420637696 | bytes 12582916 | tf_op jit(solution)/shard_map/dot_general | solution.py:25
  315.7 18.1 %reduce-scatter.7.cloned.1.call-done = f32[64,1536]{1,0:T(8,128)} async-done(((f32[512,1536]{1,0:T(8,128)}), f32[64,1536]{1,0:T(8,128)}) %reduce-scatter.7.cloned.1.call-update) | async-done | bytes 393232 | tf_op jit(solution)/shard_map/reduce_scatter | solution.py:79
  333.8 1.7 fusion.29
  335.5 40.3 %reduce-scatter.11.cloned.1.call-done = f32[64,1536]{1,0:T(8,128)} async-done(((f32[512,1536]{1,0:T(8,128)}), f32[64,1536]{1,0:T(8,128)}) %reduce-scatter.11.cloned.1.call-update) | async-done | bytes 393232 | tf_op jit(solution)/shard_map/reduce_scatter | solution.py:97
  375.8 1.4 fusion.23
  377.1 15.5 %psum.62 = f32[1536]{0:T(1024)S(1)} all-reduce(f32[1536]{0:T(1024)S(1)} %get-tuple-element.6), channel_id=1, replica_groups=mesh['row'=8,'col'=4] {'row'}, use_global_device_ids=true, to_apply=%region_19.0 | all-reduce | flops 1536 | bytes 12288 | tf_op jit(solution)/shard_map/psum | solution.py:109
  392.6 0.6 multiply_reduce_fusion.3
  393.2 9.8 %all-reduce = (f32[64]{0:T(128)S(1)}, f32[64]{0:T(128)S(1)}) all-reduce(f32[64]{0:T(128)S(1)} %get-tuple-element.7, f32[64]{0:T(128)S(1)} %get-tuple-element.8), channel_id=1, replica_groups=mesh['row'=8,'col'=4] {'col'}, use_global_device_ids=true, to_apply=%region_15.0 | all-reduce | flops 128 | bytes 1024 | tf_op jit(solution)/shard_map/psum | solution.py:101
  403.7 36.9 %psum.63 = f32[]{:T(128)} all-reduce(f32[]{:T(128)S(6)} %add.60), channel_id=1, replica_groups=mesh['row'=8,'col'=4] {'row','col'}, use_global_device_ids=true, to_apply=%region_21.0 | all-reduce | flops 1 | bytes 8 | tf_op jit(solution)/shard_map/psum | solution.py:111
  441.3 0.6 broadcast_multiply_fusion.2
  441.9 8.7 %broadcast_multiply_fusion = f32[1536,1536]{1,0:T(8,128)} fusion(f32[1536,1536]{1,0:T(8,128)} %get-tuple-element.31, f32[]{:T(128)S(6)} %min.3), kind=kLoop, calls=%fused_computation.3 | loop fusion | flops 2359296 | bytes 18874372 | tf_op jit(solution)/shard_map/mul | solution.py:116
  450.6 4.8 %broadcast_multiply_fusion.1 = f32[1536,1536]{1,0:T(8,128)} fusion(f32[1536,1536]{1,0:T(8,128)S(1)} %bitcast.12, f32[]{:T(128)S(6)} %min.3), kind=kLoop, calls=%fused_computation.4 | loop fusion | flops 2359296 | bytes 18874372 | tf_op jit(solution)/shard_map/mul | solution.py:116
  455.4 0.9 fusion.22
  (29 shorter events, 0.1 us)
Async XLA Ops:
  7.2 30.5 %all-gather.12.cloned.1.call-start = ((), (), s32[]{:S(2)}) async-start(), calls=%async_computation.9 | async-start | bytes 1769472 | tf_op jit(solution)/shard_map/all_gather | solution.py:82
  7.9 56.4 %all-gather.6.cloned.1.call-start = ((), (), s32[]{:S(2)}) async-start(), calls=%async_computation.4 | async-start | bytes 1769472 | tf_op jit(solution)/shard_map/all_gather | solution.py:45
  23.6 67.3 %all-gather.8.cloned.1.call-start = ((), (), s32[]{:S(2)}) async-start(), calls=%async_computation.5 | async-start | bytes 1769472 | tf_op jit(solution)/shard_map/all_gather | solution.py:46
  24.3 113.1 %reduce-scatter.9.cloned.1.call-start = ((), (), s32[]{:S(2)}) async-start(), calls=%async_computation.10 | async-start | bytes 3932160 | tf_op jit(solution)/shard_map/reduce_scatter | solution.py:83
  44.8 166.1 %reduce-scatter.5.cloned.1.call-start = ((), (), s32[]{:S(2)}) async-start(), calls=%async_computation.6 | async-start | bytes 7864320 | tf_op jit(solution)/shard_map/reduce_scatter | solution.py:49
  99.1 145.6 %all-gather.10.cloned.1.call-start = ((), (), s32[]{:S(2)}) async-start(), calls=%async_computation.7 | async-start | bytes 1966080 | tf_op jit(solution)/shard_map/all_gather | solution.py:75
  213.8 77.3 %all-gather.14.cloned.1.call-start = ((), (), s32[]{:S(2)}) async-start(), calls=%async_computation.11 | async-start | bytes 3932160 | tf_op jit(solution)/shard_map/all_gather | solution.py:88
  214.8 119.0 %reduce-scatter.7.cloned.1.call-start = ((), (), s32[]{:S(2)}) async-start(), calls=%async_computation.8 | async-start | bytes 3538944 | tf_op jit(solution)/shard_map/reduce_scatter | solution.py:79
  251.9 123.9 %reduce-scatter.11.cloned.1.call-start = ((), (), s32[]{:S(2)}) async-start(), calls=%async_computation.12 | async-start | bytes 3538944 | tf_op jit(solution)/shard_map/reduce_scatter | solution.py:97
  298.2 2.2 copy-start.5
  300.4 7.6 %copy-start.6 = (bf16[512,3072]{1,0:T(8,128)(2,1)S(1)}, bf16[512,3072]{1,0:T(8,128)(2,1)}, u32[]{:S(2)}) copy-start(bf16[512,3072]{1,0:T(8,128)(2,1)} %all-gather.14.cloned.1.call-done) | copy-start | bytes 9437188
  300.4 7.6 %copy-start.7 = (bf16[512,1536]{1,0:T(8,128)(2,1)S(1)}, bf16[512,1536]{1,0:T(8,128)(2,1)}, u32[]{:S(2)}) copy-start(bf16[512,1536]{1,0:T(8,128)(2,1)} %all-gather.12.cloned.1.call-done) | copy-start | bytes 4718596
  308.0 25.8 %copy-start.1 = (bf16[64,1536]{1,0:T(8,128)(2,1)S(1)}, bf16[64,1536]{1,0:T(8,128)(2,1)}, u32[]{:S(2)}) copy-start(bf16[64,1536]{1,0:T(8,128)(2,1)} %param.6) | copy-start | bytes 589828
  308.0 67.7 %copy-start = (bf16[64,1536]{1,0:T(8,128)(2,1)S(1)}, bf16[64,1536]{1,0:T(8,128)(2,1)}, u32[]{:S(2)}) copy-start(bf16[64,1536]{1,0:T(8,128)(2,1)} %param.7) | copy-start | bytes 589828
  308.0 67.7 %copy-start.4 = (f32[1536]{0:T(1024)S(1)}, f32[1536]{0:T(1024)}, u32[]{:S(2)}) copy-start(f32[1536]{0:T(1024)} %param.9) | copy-start | bytes 18436
  375.8 74.8 %slice-start = ((s8[9437184]{0:T(1024)(128)(4,1)}), s8[1048576]{0:T(1024)(128)(4,1)S(1)}, s32[]{:S(2)}) async-start(s8[9437184]{0:T(1024)(128)(4,1)} %bitcast.11), calls=%async_computation.13 | async-start | bytes 2097152
  441.9 8.7 %slice-start.1 = ((s8[9437184]{0:T(1024)(128)(4,1)}), s8[4194304]{0:T(1024)(128)(4,1)S(1)}, s32[]{:S(2)}) async-start(s8[9437184]{0:T(1024)(128)(4,1)} %bitcast.11), calls=%async_computation.14 | async-start | bytes 8388608
  441.9 8.7 %slice-start.2 = ((s8[9437184]{0:T(1024)(128)(4,1)}), s8[4194304]{0:T(1024)(128)(4,1)S(1)}, s32[]{:S(2)}) async-start(s8[9437184]{0:T(1024)(128)(4,1)} %bitcast.11), calls=%async_computation.15 | async-start | bytes 8388608
  450.6 4.8 %copy-start.2 = (f32[64,1536]{1,0:T(8,128)S(1)}, f32[64,1536]{1,0:T(8,128)}, u32[]{:S(2)}) copy-start(f32[64,1536]{1,0:T(8,128)} %reduce-scatter.11.cloned.1.call-done) | copy-start | bytes 1179652
  450.6 4.8 %copy-start.3 = (bf16[64,1536]{1,0:T(8,128)(2,1)S(1)}, bf16[64,1536]{1,0:T(8,128)(2,1)}, u32[]{:S(2)}) copy-start(bf16[64,1536]{1,0:T(8,128)(2,1)} %param.8) | copy-start | bytes 589828
Sparse Core Ops, SparseCore 0:
  9.6 27.9 all-gather.11
  39.8 24.3 all-gather.5
  66.5 24.3 all-gather.7
  94.3 43.0 reduce-scatter.8
  140.8 70.0 reduce-scatter.4
  213.9 30.8 all-gather.9
  247.2 43.8 all-gather.13
  293.4 40.3 reduce-scatter.6
  336.1 39.6 reduce-scatter.10
